TPU v7x, 32 devices: a whole 2x2x4 slice. The times are simulated.
32 devices in a mesh: row: 8 (over z, core), col: 4 (over y, x).
Axes of the slice: x: 2, y: 2, z: 4, core: 2. Of those that a mesh axis runs over, the one named last changes fastest.
Arguments:
- sky_image: bfloat16 [2, 16384, 16384], P(None, 'row', 'col'), may hold values from -6 to 6
- facet_rows: int32 [32], replicated, may hold values from 512 to 15872
- facet_offsets: int32 [32], replicated, may hold values from 0 to 511
- facet_owner: int32 [32], replicated, may hold values from 0 to 31, each once
Outputs:
- facets: bfloat16 [32, 2, 1024, 1024], P(('row', 'col'))
Inputs may be any that keep to these rules, and one draw needn't show every extreme that they name: `facet_owner`: the entries are distinct, so every device owns exactly one facet.
All inputs are finite; a program needn't handle non-finite values.
Results may differ from a plain program's by a relative error of at most 0.0095.
Values may be sent and summed in bfloat16 or wider, within the bound.
A program may use at most 320 MiB of HBM per device.

v0:
```python
import math

import jax
import jax.numpy as jnp
from jax import lax
from jax.sharding import PartitionSpec as P

N = 16384
FS = 1024
SPLIT = 128


def shifted(block, axis, distance):
    devices = range(lax.axis_size(axis))
    route = [((i - distance) % len(devices), i) for i in devices]
    return lax.ppermute(block, axis, route)


def dft_table(length):
    positions = jnp.arange(length, dtype=jnp.int32)
    turn_count = positions[:, None] * positions[None, :] % length
    angles = turn_count.astype(jnp.float32) * (-2.0 * math.pi / length)
    factor = 1.0 / math.sqrt(length)
    return (
        (jnp.cos(angles) * factor).astype(jnp.bfloat16),
        (jnp.sin(angles) * factor).astype(jnp.bfloat16),
    )


def twiddle_table(first_len, second_len, total):
    left_index = jnp.arange(first_len, dtype=jnp.int32)[:, None]
    right_index = jnp.arange(second_len, dtype=jnp.int32)[None, :]
    angles = (left_index * right_index % total).astype(jnp.float32) * (-2.0 * math.pi / total)
    return (jnp.cos(angles), jnp.sin(angles))


def paired_table(length):
    re_table, im_table = dft_table(length)
    return jnp.stack(
        (jnp.stack((re_table, -im_table), axis=1), jnp.stack((im_table, re_table), axis=1))
    )


def mix(formula, table, values):
    return jnp.einsum(formula, table, values, preferred_element_type=jnp.float32)


def rotate(pair, twiddle):
    return (
        pair[0] * twiddle[0] - pair[1] * twiddle[1],
        pair[0] * twiddle[1] + pair[1] * twiddle[0],
    )


def rows_pass(parts):
    sources, _, row_count, width = parts.shape
    lead_len = N // SPLIT
    blocks = parts.reshape(sources, 2, row_count, width // SPLIT, SPLIT)
    blocks = blocks.transpose(2, 1, 0, 3, 4).reshape(row_count, 2 * lead_len, SPLIT)
    mixed = mix("ka,rab->rkb", paired_table(lead_len).reshape(2 * lead_len, -1), blocks)
    turned = rotate((mixed[:, :lead_len], mixed[:, lead_len:]), twiddle_table(lead_len, SPLIT, N))
    section_one = jnp.concatenate([part.astype(jnp.bfloat16) for part in turned], axis=2)
    table = paired_table(SPLIT).transpose(1, 0, 2, 3).reshape(2 * SPLIT, 2 * SPLIT)
    return mix("kb,rpb->krp", table, section_one).astype(jnp.bfloat16)


def shards(sky_image, facet_rows, facet_offsets, facet_owner):
    row_devices = lax.axis_size("row")
    col_devices = lax.axis_size("col")
    devices = row_devices * col_devices
    strip_len = sky_image.shape[1] // col_devices
    parts = sky_image.reshape(2, col_devices, strip_len, -1).transpose(1, 0, 2, 3)
    parts = lax.all_to_all(parts, "col", split_axis=0, concat_axis=0, tiled=True)
    rows_done = rows_pass(parts)
    lead_len = rows_done.shape[2]
    shares = rows_done.reshape(devices, SPLIT // devices, 2, strip_len, lead_len)
    columns = lax.all_to_all(shares, ("row", "col"), split_axis=0, concat_axis=0, tiled=True)
    spans = columns.shape[1]
    col_width = spans * lead_len
    grouped = columns.transpose(1, 3, 2, 0, 4).reshape(spans, strip_len, 2 * devices, lead_len)
    mixed = mix("kg,jmgc->kjmc", paired_table(devices).reshape(2 * devices, -1), grouped)
    twiddle = twiddle_table(devices, strip_len, N)
    twiddle = (twiddle[0][:, None, :, None], twiddle[1][:, None, :, None])
    turned = rotate((mixed[:devices], mixed[devices:]), twiddle)
    section_two = jnp.concatenate([part.astype(jnp.bfloat16) for part in turned], axis=2)
    my_index = lax.axis_index(("row", "col"))
    device_ids = jnp.arange(devices, dtype=jnp.int32)
    matches = (facet_owner[None, :] == device_ids[:, None]).astype(jnp.int32)
    owned_count = jnp.sum(matches, axis=1)
    centre_row = jnp.where(owned_count > 0, jnp.sum(matches * facet_rows[None, :], axis=1), FS // 2)
    centre_col = jnp.sum(matches * facet_offsets[None, :], axis=1)
    reach_blocks = FS // (2 * col_width)
    distances = range(reach_blocks, -reach_blocks - 1, -1)
    steps = FS // devices + 1
    full_table = paired_table(strip_len).reshape(2, strip_len, -1)
    tables, heads = [], []
    for distance in distances:
        start_row = centre_row[(my_index + distance) % devices] - FS // 2
        first_step = jnp.clip(start_row // devices, 0, strip_len - steps)
        tables.append(lax.dynamic_slice_in_dim(full_table, first_step, steps, 1))
        heads.append(start_row - first_step * devices)
    table = jnp.concatenate(tables).reshape(len(tables) * 2 * steps, -1)
    bands = mix("km,pjmc->kpjc", table, section_two).astype(jnp.bfloat16)
    bands = bands.reshape(len(tables), 2, steps * devices, col_width)
    pieces = []
    for place, distance in enumerate(distances):
        band_rows = lax.dynamic_slice_in_dim(bands[place], heads[place], FS, 1)
        if distance != 0:
            band_rows = shifted(band_rows, ("row", "col"), distance)
        pieces.append(band_rows)
    window = jnp.concatenate(pieces, axis=2)
    facet_tile = lax.dynamic_slice_in_dim(window, centre_col[my_index], FS, 2)
    taper_axis = 0.25 + 0.75 * jnp.sin(math.pi * (jnp.arange(FS, dtype=jnp.float32) + 0.5) / FS)
    weight = taper_axis[:, None] * taper_axis[None, :] * owned_count[my_index].astype(jnp.float32)
    return (facet_tile.astype(jnp.float32) * weight).astype(jnp.bfloat16)[None]


def solution(mesh):
    placed = (P(None, "row", "col"), P(), P(), P())
    return jax.shard_map(
        shards,
        mesh=mesh,
        in_specs=placed,
        out_specs=P(("row", "col"), None, None, None),
        check_vma=False,
    )
```

profile of v0, /device:TPU:1, one launch (start us, length us, event | category | flops | bytes accessed | tf_op | source)
XLA Modules:
  0.0 1725.0 jit_solution(14211178928302763887)
XLA Ops:
  0.0 22.9 %copy.88 = bf16[4,2,512,4096]{3,2,1,0:T(8,128)(2,1)} copy(bf16[4,2,512,4096]{3,2,0,1:T(8,128)(2,1)} %bitcast.54) | data formatting | bytes 67108864 | tf_op jit(solution)/shard_map/transpose | solution.py:72
  22.9 9.7 all-to-all-start
  33.9 361.0 %all-to-all-done = bf16[4,2,512,4096]{3,2,1,0:T(8,128)(2,1)} async-done(((bf16[4,2,512,4096]{3,2,1,0:T(8,128)(2,1)}), bf16[4,2,512,4096]{3,2,1,0:T(8,128)(2,1)}, u32[]{:S(2)}, u32[]{:S(2)}) %all-to-all-start) | async-done | bytes 33554464 | tf_op jit(solution)/shard_map/all_to_all | solution.py:73
  394.9 41.6 %copy.89 = bf16[4,2,512,4096]{2,3,1,0:T(8,128)(2,1)} copy(bf16[4,2,512,4096]{3,2,1,0:T(8,128)(2,1)} %all-to-all-done) | data formatting | bytes 67108864 | tf_op jit(solution)/shard_map/all_to_all | solution.py:73
  436.5 54.8 %copy.90 = bf16[512,2,4,32,128]{4,3,2,1,0:T(8,128)(2,1)} copy(bf16[512,2,4,32,128]{0,4,3,1,2:T(8,128)(2,1)} %bitcast.52) | data formatting | bytes 67108864 | tf_op jit(solution)/shard_map/transpose | solution.py:59
  491.3 43.8 %copy.91 = bf16[512,256,128]{1,2,0:T(8,128)(2,1)} copy(bf16[512,256,128]{2,1,0:T(8,128)(2,1)} %bitcast.53) | data formatting | bytes 67108864 | tf_op jit(solution)/shard_map/reshape | solution.py:59
  535.1 33.2 %fusion.32 = f32[256,65536]{0,1} fusion(bf16[256,65536]{0,1:T(8,128)(2,1)} %bitcast.51, bf16[32,8,2,128]{3,2,1,0:T(2,128)(2,1)S(1)} %bitcast.58), kind=kOutput, calls=%fused_computation.55 | convolution fusion | flops 8589934592 | bytes 100794368
  568.3 33.4 %subtract_convert_fusion.1 = (bf16[512,128,128]{1,2,0:T(8,128)(2,1)}, bf16[512,128,128]{1,2,0:T(8,128)(2,1)}) fusion(f32[512,256,128]{1,2,0:T(8,128)} %bitcast.20, f32[128,128]{0,1:T(8,128)S(1)} %get-tuple-element.31, f32[128,128]{0,1:T(8,128)S(1)} %get-tuple-element.32), kind=kLoop, calls=%fused_computation.10 | loop fusion | flops 67108864 | bytes 100794368 | tf_op jit(solution)/shard_map/convert_element_type | solution.py:62
  601.7 26.6 %fusion.6 = bf16[256,512,128]{2,0,1:T(8,128)(2,1)} fusion(bf16[256,256,1]{1,0,2:T(8,128)(2,1)S(1)} %reshape.437, bf16[512,128,128]{1,2,0:T(8,128)(2,1)} %get-tuple-element.11, bf16[512,128,128]{1,2,0:T(8,128)(2,1)} %get-tuple-element.10), kind=kOutput, calls=%fused_computation.11 | convolution fusion | flops 8673820672 | bytes 67239936 | tf_op jit(solution)/shard_map/kb,rpb->krp/dot_general | solution.py:45
  628.3 27.2 %copy.93 = bf16[32,4,2,512,128]{4,2,1,3,0:T(2,128)(2,1)} copy(bf16[32,4,2,512,128]{4,2,1,0,3:T(2,128)(2,1)} %bitcast.55) | data formatting | bytes 67108864 | tf_op jit(solution)/shard_map/reshape | solution.py:76
  655.5 6.5 all-to-all-start.1
  668.9 4.4 multiply_convert_fusion.1
  679.4 756.2 %all-to-all-done.1 = bf16[32,4,2,512,128]{4,2,1,3,0:T(2,128)(2,1)} async-done(((bf16[32,4,2,512,128]{4,2,1,3,0:T(2,128)(2,1)}), bf16[32,4,2,512,128]{4,2,1,3,0:T(2,128)(2,1)}, u32[]{:S(2)}, u32[]{:S(2)}) %all-to-all-start.1) | async-done | bytes 33554464 | tf_op jit(solution)/shard_map/all_to_all | solution.py:77
  1435.7 61.8 %copy.94 = bf16[4,512,2,32,128]{4,3,2,1,0:T(8,128)(2,1)} copy(bf16[4,512,2,32,128]{4,2,0,1,3:T(2,128)(2,1)} %bitcast.23) | data formatting | bytes 67108864 | tf_op jit(solution)/shard_map/transpose | solution.py:80
  1497.5 33.2 %fusion.54 = f32[64,4,512,128]{3,0,2,1:T(8,128)} fusion(bf16[4,512,64,128]{3,2,1,0:T(8,128)(2,1)} %bitcast.50, bf16[64,64,1,1]{1,0,2,3:T(8,128)(2,1)S(1)} %reshape.438), kind=kOutput, calls=%fused_computation.94 | convolution fusion | flops 2147483648 | bytes 100671488 | tf_op jit(solution)/shard_map/kg,jmgc->kjmc/dot_general | solution.py:45
  1530.6 33.4 %subtract_convert_fusion = (bf16[32,4,512,128]{3,0,2,1:T(8,128)(2,1)}, bf16[32,4,512,128]{3,0,2,1:T(8,128)(2,1)}) fusion(f32[64,4,512,128]{3,0,2,1:T(8,128)} %fusion.54, f32[32,512]{0,1:T(8,128)S(1)} %get-tuple-element.35, f32[32,512]{0,1:T(8,128)S(1)} %get-tuple-element.36), kind=kLoop, calls=%fused_computation.8 | loop fusion | flops 67108864 | bytes 100794368 | tf_op jit(solution)/shard_map/convert_element_type | solution.py:85
  1564.1 23.2 %pad_maximum_fusion = bf16[32,4,1024,128]{3,0,2,1:T(8,128)(2,1)} fusion(bf16[32,4,512,128]{3,0,2,1:T(8,128)(2,1)} %get-tuple-element.9, bf16[32,4,512,128]{3,0,2,1:T(8,128)(2,1)} %get-tuple-element.8), kind=kLoop, calls=%fused_computation.4 | loop fusion | flops 16777216 | bytes 67108864 | tf_op jit(solution)/shard_map/concatenate | solution.py:85
  1587.3 31.5 %fusion.9 = bf16[198,32,4,128]{3,0,2,1:T(8,128)(2,1)S(1)} fusion(bf16[32,4,1024,128]{3,0,2,1:T(8,128)(2,1)} %pad_maximum_fusion, bf16[198,1024,1,1]{1,0,2,3:T(8,128)(2,1)S(1)} %reshape.439), kind=kOutput, calls=%fused_computation.13 | convolution fusion | flops 6647021568 | bytes 40448000 | tf_op jit(solution)/shard_map/km,pjmc->kpjc/dot_general | solution.py:45
  1618.8 4.4 fusion.63
  1625.7 4.7 squeeze.16
  1638.1 4.7 squeeze.18
  1661.8 32.1 %collective-permute-done = bf16[2,1024,512]{2,1,0:T(8,128)(2,1)} collective-permute-done((bf16[2,1024,512]{2,1,0:T(8,128)(2,1)}, bf16[2,1024,512]{2,1,0:T(8,128)(2,1)}, u32[]{:S(2)}, u32[]{:S(2)}) %collective-permute-start) | collective-permute-done | bytes 2097184 | tf_op jit(solution)/shard_map/ppermute | solution.py:16
  1693.8 22.6 %collective-permute-done.1 = bf16[2,1024,512]{2,1,0:T(8,128)(2,1)} collective-permute-done((bf16[2,1024,512]{2,1,0:T(8,128)(2,1)}, bf16[2,1024,512]{2,1,0:T(8,128)(2,1)}, u32[]{:S(2)}, u32[]{:S(2)}) %collective-permute-start.1) | collective-permute-done | bytes 2097184 | tf_op jit(solution)/shard_map/ppermute | solution.py:16
  1716.4 8.1 fusion.14
  (47 shorter events, 38.8 us)
Async XLA Ops:
  22.9 372.0 %all-to-all-start = ((bf16[4,2,512,4096]{3,2,1,0:T(8,128)(2,1)}), bf16[4,2,512,4096]{3,2,1,0:T(8,128)(2,1)}, u32[]{:S(2)}, u32[]{:S(2)}) async-start(bf16[4,2,512,4096]{3,2,1,0:T(8,128)(2,1)} %copy.88), calls=%async_computation | async-start | bytes 67108864 | tf_op jit(solution)/shard_map/all_to_all | solution.py:73
  655.5 6.6 copy-start
  655.5 6.6 copy-start.1
  655.5 6.6 copy-start.2
  655.5 780.1 %all-to-all-start.1 = ((bf16[32,4,2,512,128]{4,2,1,3,0:T(2,128)(2,1)}), bf16[32,4,2,512,128]{4,2,1,3,0:T(2,128)(2,1)}, u32[]{:S(2)}, u32[]{:S(2)}) async-start(bf16[32,4,2,512,128]{4,2,1,3,0:T(2,128)(2,1)} %copy.93), calls=%async_computation.1 | async-start | bytes 67108864 | tf_op jit(solution)/shard_map/all_to_all | solution.py:77
  1633.8 60.0 %collective-permute-start = (bf16[2,1024,512]{2,1,0:T(8,128)(2,1)}, bf16[2,1024,512]{2,1,0:T(8,128)(2,1)}, u32[]{:S(2)}, u32[]{:S(2)}) collective-permute-start(bf16[2,1024,512]{2,1,0:T(8,128)(2,1)} %constant_dynamic-slice_fusion.2), channel_id=1, source_target_pairs={{31,0},{0,1},{1,2},{2,3},{3,4},{4,5},{5,6},{6,7},{7,8},{8,9},{9,10... | collective-permute-start | bytes 6291464 | tf_op jit(solution)/shard_map/ppermute | solution.py:16
  1646.1 70.3 %collective-permute-start.1 = (bf16[2,1024,512]{2,1,0:T(8,128)(2,1)}, bf16[2,1024,512]{2,1,0:T(8,128)(2,1)}, u32[]{:S(2)}, u32[]{:S(2)}) collective-permute-start(bf16[2,1024,512]{2,1,0:T(8,128)(2,1)} %constant_dynamic-slice_fusion), channel_id=1, source_target_pairs={{1,0},{2,1},{3,2},{4,3},{5,4},{6,5},{7,6},{8,7},{9,8},{10,9},{11,1... | collective-permute-start | bytes 6291464 | tf_op jit(solution)/shard_map/ppermute | solution.py:16
where the time goes:
time: 1740 us; the launch traced here: 1720 us
  waiting for transfers between devices  1170 us (67%)
  local copies, waits for them, and re-layouts  292 us (17%)
  matrix products  124 us (7%)
  other arithmetic  113 us (6%)
  starting transfers between devices  18.9 us (1%)
    all_to_all x1, waiting for transfers between devices, shards(): lax.all_to_all(shares, ('row', 'col'), split_axis=0, concat_axis=0, tiled...  756 us
    all_to_all x1, waiting for transfers between devices, shards(): lax.all_to_all(parts, 'col', split_axis=0, concat_axis=0, tiled=True)  361 us
    dot_general x3, matrix products, mix(): jnp.einsum(formula, table, values, preferred_element_type=jnp.float32)  91.3 us
    transpose x1, local copies, waits for them, and re-layouts, shards(): columns.transpose(1, 3, 2, 0, 4)  61.8 us
    transpose x1, local copies, waits for them, and re-layouts, rows_pass(): blocks.transpose(2, 1, 0, 3, 4).reshape(row_count, 2 * lead_len, SPLIT)  54.8 us
    ppermute x2, waiting for transfers between devices, shifted(): return lax.ppermute(block, axis, route)  54.6 us
    reshape x1, local copies, waits for them, and re-layouts, rows_pass(): blocks.transpose(2, 1, 0, 3, 4).reshape(row_count, 2 * lead_len, SPLIT)  43.8 us
    all_to_all x1, local copies, waits for them, and re-layouts, shards(): lax.all_to_all(parts, 'col', split_axis=0, concat_axis=0, tiled=True)  41.6 us
  transfers between devices with their start and end apart: 4, of which 4 were waited for; matrix products, arithmetic and copies ran while one was open for 2% of the time, Pallas kernels for 0%

commit v1 on v0

v1 whole, which is shorter than its diff:
```python
import math

import jax
import jax.numpy as jnp
from jax import lax
from jax.sharding import PartitionSpec as P


N = 16384
FS = 1024
SPLIT = 128
PARTS = (1, 2, 2, 2, 1)
AHEAD = 2


def shifted(block, axis, distance):
    devices = range(lax.axis_size(axis))
    route = [((i - distance) % len(devices), i) for i in devices]
    return lax.ppermute(block, axis, route)


def dft_table(length):
    positions = jnp.arange(length, dtype=jnp.int32)
    turn_count = positions[:, None] * positions[None, :] % length
    angles = turn_count.astype(jnp.float32) * (-2.0 * math.pi / length)
    factor = 1.0 / math.sqrt(length)
    return (
        (jnp.cos(angles) * factor).astype(jnp.bfloat16),
        (jnp.sin(angles) * factor).astype(jnp.bfloat16),
    )


def twiddle_table(first_len, second_len, total):
    left_index = jnp.arange(first_len, dtype=jnp.int32)[:, None]
    right_index = jnp.arange(second_len, dtype=jnp.int32)[None, :]
    angles = (left_index * right_index % total).astype(jnp.float32) * (-2.0 * math.pi / total)
    return (jnp.cos(angles), jnp.sin(angles))


def paired_table(length):
    re_table, im_table = dft_table(length)
    return jnp.stack(
        (jnp.stack((re_table, -im_table), axis=1), jnp.stack((im_table, re_table), axis=1))
    )


def mix(formula, table, values):
    return jnp.einsum(formula, table, values, preferred_element_type=jnp.float32)


def rotate(pair, twiddle):
    return (
        pair[0] * twiddle[0] - pair[1] * twiddle[1],
        pair[0] * twiddle[1] + pair[1] * twiddle[0],
    )


def rows_pass(parts, order, devices):
    sources, _, row_count, width = parts.shape
    lead_len = N // SPLIT
    blocks = parts.reshape(sources, 2, row_count, width // SPLIT, SPLIT)
    blocks = blocks.transpose(2, 1, 0, 3, 4).reshape(row_count, 2 * lead_len, SPLIT)
    first = paired_table(lead_len).reshape(2 * lead_len, 2, sources, -1)
    first = jnp.take(first, order, axis=2).reshape(2 * lead_len, -1)
    mixed = mix("ka,rab->rkb", first, blocks)
    turned = rotate((mixed[:, :lead_len], mixed[:, lead_len:]), twiddle_table(lead_len, SPLIT, N))
    section_one = jnp.concatenate([part.astype(jnp.bfloat16) for part in turned], axis=2)
    table = paired_table(SPLIT).transpose(1, 0, 2, 3).reshape(2 * SPLIT, 2 * SPLIT)
    done = mix("kb,rpb->rkp", table, section_one).astype(jnp.bfloat16)
    return done.reshape(row_count, devices, -1, lead_len).transpose(1, 0, 2, 3)


def strip_table(devices, spans):
    pairs = paired_table(devices)
    eye = jnp.eye(spans, dtype=jnp.bfloat16)
    full = pairs.transpose(0, 1, 3, 2)[:, None, :, :, None, :] * eye[None, :, None, None, :, None]
    return full.reshape(2 * spans * devices, devices, spans * 2)


def shards(sky_image, facet_rows, facet_offsets, facet_owner):
    row_devices = lax.axis_size("row")
    col_devices = lax.axis_size("col")
    devices = row_devices * col_devices
    strip_len = sky_image.shape[1] // col_devices
    sizes = [part * strip_len // sum(PARTS) for part in PARTS]
    starts = [sum(sizes[:place]) for place in range(len(sizes))]
    my_index = lax.axis_index(("row", "col"))
    device_ids = jnp.arange(devices, dtype=jnp.int32)
    matches = (facet_owner[None, :] == device_ids[:, None]).astype(jnp.int32)
    owned_count = jnp.sum(matches, axis=1)
    centre_row = jnp.where(owned_count > 0, jnp.sum(matches * facet_rows[None, :], axis=1), FS // 2)
    centre_col = jnp.sum(matches * facet_offsets[None, :], axis=1)

    lead_len = N // SPLIT
    spans = SPLIT // devices
    col_width = spans * lead_len
    reach_blocks = FS // (2 * col_width)
    distances = range(reach_blocks, -reach_blocks - 1, -1)
    steps = FS // devices + 1
    full_table = paired_table(strip_len).reshape(2, strip_len, 2, strip_len)
    tables, heads = [], []
    for distance in distances:
        start_row = centre_row[(my_index + distance) % devices] - FS // 2
        first_step = jnp.clip(start_row // devices, 0, strip_len - steps)
        tables.append(lax.dynamic_slice_in_dim(full_table, first_step, steps, 1))
        heads.append(start_row - first_step * devices)
    sides = [place for place, distance in enumerate(distances) if distance != 0]
    groups = [sides, [len(sides) // 2]]
    group_tables = [
        jnp.concatenate([tables[place] for place in group]).reshape(-1, 2, strip_len)
        for group in groups
    ]
    full_twiddle = twiddle_table(devices, strip_len, N)

    my_col = lax.axis_index("col")
    order = my_col ^ jnp.arange(col_devices, dtype=jnp.int32)
    image = sky_image.reshape(2, col_devices, strip_len, -1)

    def fetch(place, after):
        here = my_col
        if after is not None:
            here = lax.optimization_barrier((here, after))[0]
        pieces = []
        for hop in range(col_devices):
            sent = lax.dynamic_slice(
                image, (0, here ^ hop, starts[place], 0), (2, 1, sizes[place], image.shape[3])
            )[:, 0]
            if hop:
                sent = lax.ppermute(sent, "col", [(i, i ^ hop) for i in range(col_devices)])
            pieces.append(sent)
        return pieces

    strips = strip_table(devices, spans).reshape(2 * spans * devices, devices, -1)

    def columns_pass(columns, place):
        mixed = mix("ugs,grsp->rup", strips, columns)
        half = spans * devices
        band = slice(starts[place], starts[place] + sizes[place])
        twiddle = tuple(jnp.tile(t[:, band].T, (1, spans))[:, :, None] for t in full_twiddle)
        turned = rotate((mixed[:, :half], mixed[:, half:]), twiddle)
        section_two = jnp.concatenate([part.astype(jnp.bfloat16) for part in turned], axis=0)
        section_two = section_two.reshape(-1, spans, devices, lead_len)
        return [
            mix("km,mjpc->kpjc", t[:, :, band].reshape(t.shape[0], -1), section_two)
            for t in group_tables
        ]

    count = len(sizes)
    totals, spread, gate = None, [], None
    queue = [fetch(0, None), fetch(1, None)]

    def gather_columns(place, totals):
        columns = spread[place]
        if totals is not None:
            columns, totals = lax.optimization_barrier((columns, totals))
        fresh = columns_pass(columns, place)
        if totals is None:
            return fresh
        return [old + new for old, new in zip(totals, fresh)]

    for place in range(count):
        got = queue.pop(0)
        if gate is not None:
            got = list(lax.optimization_barrier((*got, gate))[:-1])
        shares = rows_pass(jnp.stack(got), order, devices)
        if totals is not None:
            shares, totals = lax.optimization_barrier((shares, totals))
        gate = shares
        if place + AHEAD < count:
            queue.append(fetch(place + AHEAD, gate))
        spread.append(
            lax.all_to_all(shares, ("row", "col"), split_axis=0, concat_axis=0, tiled=True)
        )
        if place >= 1:
            totals = gather_columns(place - 1, totals)
    totals = gather_columns(count - 1, totals)
    pieces = [None] * len(tables)
    for group, total in zip(groups, totals):
        bands = total.astype(jnp.bfloat16).reshape(len(group), 2, steps * devices, col_width)
        for spot, place in enumerate(group):
            band_rows = lax.dynamic_slice_in_dim(bands[spot], heads[place], FS, 1)
            if distances[place] != 0:
                band_rows = shifted(band_rows, ("row", "col"), distances[place])
            pieces[place] = band_rows
    window = jnp.concatenate(pieces, axis=2)
    facet_tile = lax.dynamic_slice_in_dim(window, centre_col[my_index], FS, 2)
    taper_axis = 0.25 + 0.75 * jnp.sin(math.pi * (jnp.arange(FS, dtype=jnp.float32) + 0.5) / FS)
    weight = taper_axis[:, None] * taper_axis[None, :] * owned_count[my_index].astype(jnp.float32)
    return (facet_tile.astype(jnp.float32) * weight).astype(jnp.bfloat16)[None]


def solution(mesh):
    placed = (P(None, "row", "col"), P(), P(), P())
    return jax.shard_map(
        shards,
        mesh=mesh,
        in_specs=placed,
        out_specs=P(("row", "col"), None, None, None),
        check_vma=False,
    )
```

time: 1740 us -> 1300 us (0.75)
  waiting for transfers between devices: 1170 us -> 736 us
  local copies, waits for them, and re-layouts: 292 us -> 227 us
  starting transfers between devices: 18.9 us -> 69 us
  matrix products: 124 us -> 157 us
  other arithmetic: 113 us -> 90.1 us
    all_to_all x1 -> x5, waiting for transfers between devices: 756 us -> 33.7 us  [shards(): lax.all_to_all(shares, ('row', 'col'), split_axis=0, concat_axis=0, tiled...]
    ppermute x0 -> x15, waiting for transfers between devices: none -> 639 us  [fetch(): sent = lax.ppermute(sent, 'col', [(i, i ^ hop) for i in range(col_devices)])]
    all_to_all x1 -> x0, waiting for transfers between devices: 361 us -> none  [shards(): lax.all_to_all(parts, 'col', split_axis=0, concat_axis=0, tiled=True)]
    transpose x3 -> x7, local copies, waits for them, and re-layouts: 139 us -> 16 us  [the longest x2 14.4 us: rows_pass(): return done.reshape(row_count, devices, -1, lead_len).transpose(1, 0, 2, 3)]
    dot_general x3 -> x25, matrix products: 91.3 us -> 157 us  [mix(): jnp.einsum(formula, table, values, preferred_element_type=jnp.float32)]
    convert_element_type x0 -> x6, local copies, waits for them, and re-layouts: none -> 50.5 us  [the longest x5 48.8 us: rows_pass(): done = mix('kb,rpb->rkp', table, section_one).astype(jnp.bfloat16)]
    all_to_all x1 -> x5, starting transfers between devices: 6.51 us -> 52.3 us  [shards(): lax.all_to_all(shares, ('row', 'col'), split_axis=0, concat_axis=0, tiled...]
    all_to_all x1 -> x0, local copies, waits for them, and re-layouts: 41.6 us -> none  [shards(): lax.all_to_all(parts, 'col', split_axis=0, concat_axis=0, tiled=True)]
  transfers between devices with their start and end apart: 4 -> 22, of which waited for: 4 -> 16; matrix products, arithmetic and copies ran while one was open for 2% -> 32% of each run, Pallas kernels for 0% -> 0%
where the time goes in v1:
time: 1300 us; the launch traced here: 1280 us
  waiting for transfers between devices  736 us (57%)
  local copies, waits for them, and re-layouts  227 us (17%)
  matrix products  157 us (12%)
  other arithmetic  90.1 us (7%)
  starting transfers between devices  69 us (5%)
    ppermute x15, waiting for transfers between devices, fetch(): sent = lax.ppermute(sent, 'col', [(i, i ^ hop) for i in range(col_devices)])  639 us
    dot_general x25, matrix products, mix(): jnp.einsum(formula, table, values, preferred_element_type=jnp.float32)  157 us
    ppermute x2, waiting for transfers between devices, shifted(): return lax.ppermute(block, axis, route)  63 us
    all_to_all x5, starting transfers between devices, shards(): lax.all_to_all(shares, ('row', 'col'), split_axis=0, concat_axis=0, tiled...  52.3 us
    reshape x5, local copies, waits for them, and re-layouts, columns_pass(): section_two = section_two.reshape(-1, spans, devices, lead_len)  48.9 us
    convert_element_type x5, local copies, waits for them, and re-layouts, rows_pass(): done = mix('kb,rpb->rkp', table, section_one).astype(jnp.bfloat16)  48.8 us
    all_to_all x5, waiting for transfers between devices, shards(): lax.all_to_all(shares, ('row', 'col'), split_axis=0, concat_axis=0, tiled...  33.7 us
    unnamed x56, local copies, waits for them, and re-layouts  33.6 us
  transfers between devices with their start and end apart: 22, of which 16 were waited for; matrix products, arithmetic and copies ran while one was open for 32% of the time, Pallas kernels for 0%

profile of v1, /device:TPU:1, one launch (start us, length us, event | category | flops | bytes accessed | tf_op | source)
XLA Modules:
  0.0 1284.9 jit_solution(16634089925156191801)
XLA Ops:
  10.0 18.8 %collective-permute-done = bf16[2,64,4096]{2,1,0:T(8,128)(2,1)} collective-permute-done((bf16[2,64,4096]{2,1,0:T(8,128)(2,1)}, bf16[2,64,4096]{2,1,0:T(8,128)(2,1)}, u32[]{:S(2)}, u32[]{:S(2)}) %collective-permute-start) | collective-permute-done | bytes 1048608 | tf_op jit(solution)/shard_map/ppermute | solution.py:129
  31.7 20.5 %collective-permute-done.2 = bf16[2,64,4096]{2,1,0:T(8,128)(2,1)} collective-permute-done((bf16[2,64,4096]{2,1,0:T(8,128)(2,1)S(1)}, bf16[2,64,4096]{2,1,0:T(8,128)(2,1)}, u32[]{:S(2)}, u32[]{:S(2)}) %collective-permute-start.2) | collective-permute-done | bytes 1048608 | tf_op jit(solution)/shard_map/ppermute | solution.py:129
  87.3 84.6 %collective-permute-done.6 = bf16[2,128,4096]{2,1,0:T(8,128)(2,1)S(1)} collective-permute-done((bf16[2,128,4096]{2,1,0:T(8,128)(2,1)S(1)}, bf16[2,128,4096]{2,1,0:T(8,128)(2,1)S(1)}, u32[]{:S(2)}, u32[]{:S(2)}) %collective-permute-start.6) | collective-permute-done | bytes 2097184 | tf_op jit(solution)/shard_map/ppermute | solution.py:129
  172.6 45.7 %collective-permute-done.8 = bf16[2,128,4096]{2,1,0:T(8,128)(2,1)S(1)} collective-permute-done((bf16[2,128,4096]{2,1,0:T(8,128)(2,1)S(1)}, bf16[2,128,4096]{2,1,0:T(8,128)(2,1)S(1)}, u32[]{:S(2)}, u32[]{:S(2)}) %collective-permute-start.8) | collective-permute-done | bytes 2097184 | tf_op jit(solution)/shard_map/ppermute | solution.py:129
  236.5 11.9 copy.337
  269.9 11.5 dynamic-slice_bitcast_fusion
  297.8 95.8 %collective-permute-done.3 = bf16[2,128,4096]{2,1,0:T(8,128)(2,1)} collective-permute-done((bf16[2,128,4096]{2,1,0:T(8,128)(2,1)}, bf16[2,128,4096]{2,1,0:T(8,128)(2,1)}, u32[]{:S(2)}, u32[]{:S(2)}) %collective-permute-start.3) | collective-permute-done | bytes 2097184 | tf_op jit(solution)/shard_map/ppermute | solution.py:129
  401.5 52.3 %collective-permute-done.5 = bf16[2,128,4096]{2,1,0:T(8,128)(2,1)} collective-permute-done((bf16[2,128,4096]{2,1,0:T(8,128)(2,1)}, bf16[2,128,4096]{2,1,0:T(8,128)(2,1)}, u32[]{:S(2)}, u32[]{:S(2)}) %collective-permute-start.5) | collective-permute-done | bytes 2097184 | tf_op jit(solution)/shard_map/ppermute | solution.py:129
  478.8 12.3 copy.340
  524.6 12.5 all-to-all-start.2
  540.8 123.6 %collective-permute-done.12 = bf16[2,128,4096]{2,1,0:T(8,128)(2,1)} collective-permute-done((bf16[2,128,4096]{2,1,0:T(8,128)(2,1)}, bf16[2,128,4096]{2,1,0:T(8,128)(2,1)}, u32[]{:S(2)}, u32[]{:S(2)}) %collective-permute-start.12) | collective-permute-done | bytes 2097184 | tf_op jit(solution)/shard_map/ppermute | solution.py:129
  672.3 52.3 %collective-permute-done.14 = bf16[2,128,4096]{2,1,0:T(8,128)(2,1)} collective-permute-done((bf16[2,128,4096]{2,1,0:T(8,128)(2,1)}, bf16[2,128,4096]{2,1,0:T(8,128)(2,1)}, u32[]{:S(2)}, u32[]{:S(2)}) %collective-permute-start.14) | collective-permute-done | bytes 2097184 | tf_op jit(solution)/shard_map/ppermute | solution.py:129
  740.9 11.9 copy.352
  752.8 12.6 convolution_bitcast_fusion.2
  782.6 11.7 copy.419
  821.0 12.1 all-to-all-start.4
  840.1 118.8 %collective-permute-done.10 = bf16[2,64,4096]{2,1,0:T(8,128)(2,1)} collective-permute-done((bf16[2,64,4096]{2,1,0:T(8,128)(2,1)}, bf16[2,64,4096]{2,1,0:T(8,128)(2,1)}, u32[]{:S(2)}, u32[]{:S(2)}) %collective-permute-start.10) | collective-permute-done | bytes 1048608 | tf_op jit(solution)/shard_map/ppermute | solution.py:129
  986.0 12.6 convolution_bitcast_fusion.1
  1015.4 11.8 copy.423
  1059.6 12.6 convolution_bitcast_fusion
  1089.1 11.8 copy.425
  1118.6 33.7 %all-to-all-done.3 = bf16[32,64,8,128]{3,2,1,0:T(8,128)(2,1)} async-done(((bf16[32,64,8,128]{3,2,1,0:T(8,128)(2,1)}), bf16[32,64,8,128]{3,2,1,0:T(8,128)(2,1)}, u32[]{:S(2)}, u32[]{:S(2)}) %all-to-all-start.3) | async-done | bytes 4194336 | tf_op jit(solution)/shard_map/all_to_all | solution.py:172
  1214.2 39.7 %collective-permute-done.15 = bf16[2,1024,512]{2,1,0:T(8,128)(2,1)} collective-permute-done((bf16[2,1024,512]{2,1,0:T(8,128)(2,1)}, bf16[2,1024,512]{2,1,0:T(8,128)(2,1)}, u32[]{:S(2)}, u32[]{:S(2)}) %collective-permute-start.15) | collective-permute-done | bytes 2097184 | tf_op jit(solution)/shard_map/ppermute | solution.py:19
  1253.9 23.3 %collective-permute-done.16 = bf16[2,1024,512]{2,1,0:T(8,128)(2,1)} collective-permute-done((bf16[2,1024,512]{2,1,0:T(8,128)(2,1)}, bf16[2,1024,512]{2,1,0:T(8,128)(2,1)}, u32[]{:S(2)}, u32[]{:S(2)}) %collective-permute-start.16) | collective-permute-done | bytes 2097184 | tf_op jit(solution)/shard_map/ppermute | solution.py:19
  (223 shorter events, 424.5 us)
Async XLA Ops:
  3.5 25.2 %collective-permute-start = (bf16[2,64,4096]{2,1,0:T(8,128)(2,1)}, bf16[2,64,4096]{2,1,0:T(8,128)(2,1)}, u32[]{:S(2)}, u32[]{:S(2)}) collective-permute-start(bf16[2,64,4096]{2,1,0:T(8,128)(2,1)} %get-tuple-element.108), channel_id=1, source_target_pairs={{0,1},{1,0},{2,3},{3,2},{4,5},{5,4},{6,7},{7,6},{8,9},{9,8},{10,11... | collective-permute-start | bytes 3145736 | tf_op jit(solution)/shard_map/ppermute | solution.py:129
  5.6 24.6 %collective-permute-start.1 = (bf16[2,64,4096]{2,1,0:T(8,128)(2,1)S(1)}, bf16[2,64,4096]{2,1,0:T(8,128)(2,1)}, u32[]{:S(2)}, u32[]{:S(2)}) collective-permute-start(bf16[2,64,4096]{2,1,0:T(8,128)(2,1)S(1)} %get-tuple-element.107), channel_id=1, source_target_pairs={{0,2},{1,3},{2,0},{3,1},{4,6},{5,7},{6,4},{7,5},{8,10},{9,11},{10,... | collective-permute-start | bytes 3145736 | tf_op jit(solution)/shard_map/ppermute | solution.py:129
  6.8 45.3 %collective-permute-start.2 = (bf16[2,64,4096]{2,1,0:T(8,128)(2,1)S(1)}, bf16[2,64,4096]{2,1,0:T(8,128)(2,1)}, u32[]{:S(2)}, u32[]{:S(2)}) collective-permute-start(bf16[2,64,4096]{2,1,0:T(8,128)(2,1)S(1)} %get-tuple-element.106), channel_id=1, source_target_pairs={{0,3},{1,2},{2,1},{3,0},{4,7},{5,6},{6,5},{7,4},{8,11},{9,10},{10,... | collective-permute-start | bytes 3145736 | tf_op jit(solution)/shard_map/ppermute | solution.py:129
  72.4 184.9 %all-to-all-start = ((bf16[32,64,8,128]{3,2,1,0:T(8,128)(2,1)}), bf16[32,64,8,128]{3,2,1,0:T(8,128)(2,1)}, u32[]{:S(2)}, u32[]{:S(2)}) async-start(bf16[32,64,8,128]{3,2,1,0:T(8,128)(2,1)} %copy.341), calls=%async_computation | async-start | bytes 8388608 | tf_op jit(solution)/shard_map/all_to_all | solution.py:172
  84.6 87.3 %collective-permute-start.6 = (bf16[2,128,4096]{2,1,0:T(8,128)(2,1)S(1)}, bf16[2,128,4096]{2,1,0:T(8,128)(2,1)S(1)}, u32[]{:S(2)}, u32[]{:S(2)}) collective-permute-start(bf16[2,128,4096]{2,1,0:T(8,128)(2,1)S(1)} %get-tuple-element.103), channel_id=1, source_target_pairs={{0,1},{1,0},{2,3},{3,2},{4,5},{5,4},{6,7},{7,6},{8,9},{9,8},{10,11... | collective-permute-start | bytes 6291464 | tf_op jit(solution)/shard_map/ppermute | solution.py:129
  86.0 86.5 %collective-permute-start.7 = (bf16[2,128,4096]{2,1,0:T(8,128)(2,1)S(1)}, bf16[2,128,4096]{2,1,0:T(8,128)(2,1)S(1)}, u32[]{:S(2)}, u32[]{:S(2)}) collective-permute-start(bf16[2,128,4096]{2,1,0:T(8,128)(2,1)S(1)} %get-tuple-element.102), channel_id=1, source_target_pairs={{0,2},{1,3},{2,0},{3,1},{4,6},{5,7},{6,4},{7,5},{8,10},{9,11},{10,... | collective-permute-start | bytes 6291464 | tf_op jit(solution)/shard_map/ppermute | solution.py:129
  87.2 131.1 %collective-permute-start.8 = (bf16[2,128,4096]{2,1,0:T(8,128)(2,1)S(1)}, bf16[2,128,4096]{2,1,0:T(8,128)(2,1)S(1)}, u32[]{:S(2)}, u32[]{:S(2)}) collective-permute-start(bf16[2,128,4096]{2,1,0:T(8,128)(2,1)S(1)} %get-tuple-element.101), channel_id=1, source_target_pairs={{0,3},{1,2},{2,1},{3,0},{4,7},{5,6},{6,5},{7,4},{8,11},{9,10},{10,... | collective-permute-start | bytes 6291464 | tf_op jit(solution)/shard_map/ppermute | solution.py:129
  257.4 267.2 %all-to-all-start.1 = ((bf16[32,128,8,128]{3,2,1,0:T(8,128)(2,1)}), bf16[32,128,8,128]{3,2,1,0:T(8,128)(2,1)}, u32[]{:S(2)}, u32[]{:S(2)}) async-start(bf16[32,128,8,128]{3,2,1,0:T(8,128)(2,1)} %copy.353), calls=%async_computation.1 | async-start | bytes 16777216 | tf_op jit(solution)/shard_map/all_to_all | solution.py:172
  267.0 14.4 %copy-start.16 = (s32[32]{0:T(128)}, s32[32]{0:T(128)S(1)}, u32[]{:S(2)}) copy-start(s32[32]{0:T(128)S(1)} %get-tuple-element.88) | copy-start | bytes 388
  281.4 112.2 %collective-permute-start.3 = (bf16[2,128,4096]{2,1,0:T(8,128)(2,1)}, bf16[2,128,4096]{2,1,0:T(8,128)(2,1)}, u32[]{:S(2)}, u32[]{:S(2)}) collective-permute-start(bf16[2,128,4096]{2,1,0:T(8,128)(2,1)} %get-tuple-element.95), channel_id=1, source_target_pairs={{0,1},{1,0},{2,3},{3,2},{4,5},{5,4},{6,7},{7,6},{8,9},{9,8},{10,11... | collective-permute-start | bytes 6291464 | tf_op jit(solution)/shard_map/ppermute | solution.py:129
  282.8 118.7 %collective-permute-start.4 = (bf16[2,128,4096]{2,1,0:T(8,128)(2,1)}, bf16[2,128,4096]{2,1,0:T(8,128)(2,1)}, u32[]{:S(2)}, u32[]{:S(2)}) collective-permute-start(bf16[2,128,4096]{2,1,0:T(8,128)(2,1)} %get-tuple-element.94), channel_id=1, source_target_pairs={{0,2},{1,3},{2,0},{3,1},{4,6},{5,7},{6,4},{7,5},{8,10},{9,11},{10,... | collective-permute-start | bytes 6291464 | tf_op jit(solution)/shard_map/ppermute | solution.py:129
  284.0 169.8 %collective-permute-start.5 = (bf16[2,128,4096]{2,1,0:T(8,128)(2,1)}, bf16[2,128,4096]{2,1,0:T(8,128)(2,1)}, u32[]{:S(2)}, u32[]{:S(2)}) collective-permute-start(bf16[2,128,4096]{2,1,0:T(8,128)(2,1)} %get-tuple-element.93), channel_id=1, source_target_pairs={{0,3},{1,2},{2,1},{3,0},{4,7},{5,6},{6,5},{7,4},{8,11},{9,10},{10,... | collective-permute-start | bytes 6291464 | tf_op jit(solution)/shard_map/ppermute | solution.py:129
  524.6 296.4 %all-to-all-start.2 = ((bf16[32,128,8,128]{3,2,1,0:T(8,128)(2,1)}), bf16[32,128,8,128]{3,2,1,0:T(8,128)(2,1)}, u32[]{:S(2)}, u32[]{:S(2)}) async-start(bf16[32,128,8,128]{3,2,1,0:T(8,128)(2,1)} %copy.362), calls=%async_computation.2 | async-start | bytes 16777216 | tf_op jit(solution)/shard_map/all_to_all | solution.py:172
  537.1 127.3 %collective-permute-start.12 = (bf16[2,128,4096]{2,1,0:T(8,128)(2,1)}, bf16[2,128,4096]{2,1,0:T(8,128)(2,1)}, u32[]{:S(2)}, u32[]{:S(2)}) collective-permute-start(bf16[2,128,4096]{2,1,0:T(8,128)(2,1)} %get-tuple-element.91), channel_id=1, source_target_pairs={{0,1},{1,0},{2,3},{3,2},{4,5},{5,4},{6,7},{7,6},{8,9},{9,8},{10,11... | collective-permute-start | bytes 6291464 | tf_op jit(solution)/shard_map/ppermute | solution.py:129
  538.5 133.8 %collective-permute-start.13 = (bf16[2,128,4096]{2,1,0:T(8,128)(2,1)}, bf16[2,128,4096]{2,1,0:T(8,128)(2,1)}, u32[]{:S(2)}, u32[]{:S(2)}) collective-permute-start(bf16[2,128,4096]{2,1,0:T(8,128)(2,1)} %get-tuple-element.90), channel_id=1, source_target_pairs={{0,2},{1,3},{2,0},{3,1},{4,6},{5,7},{6,4},{7,5},{8,10},{9,11},{10,... | collective-permute-start | bytes 6291464 | tf_op jit(solution)/shard_map/ppermute | solution.py:129
  539.7 184.9 %collective-permute-start.14 = (bf16[2,128,4096]{2,1,0:T(8,128)(2,1)}, bf16[2,128,4096]{2,1,0:T(8,128)(2,1)}, u32[]{:S(2)}, u32[]{:S(2)}) collective-permute-start(bf16[2,128,4096]{2,1,0:T(8,128)(2,1)} %get-tuple-element.89), channel_id=1, source_target_pairs={{0,3},{1,2},{2,1},{3,0},{4,7},{5,6},{6,5},{7,4},{8,11},{9,10},{10,... | collective-permute-start | bytes 6291464 | tf_op jit(solution)/shard_map/ppermute | solution.py:129
  821.0 227.2 %all-to-all-start.4 = ((bf16[32,128,8,128]{3,2,1,0:T(8,128)(2,1)}), bf16[32,128,8,128]{3,2,1,0:T(8,128)(2,1)}, u32[]{:S(2)}, u32[]{:S(2)}) async-start(bf16[32,128,8,128]{3,2,1,0:T(8,128)(2,1)} %copy.369), calls=%async_computation.4 | async-start | bytes 16777216 | tf_op jit(solution)/shard_map/all_to_all | solution.py:172
  837.1 121.8 %collective-permute-start.10 = (bf16[2,64,4096]{2,1,0:T(8,128)(2,1)}, bf16[2,64,4096]{2,1,0:T(8,128)(2,1)}, u32[]{:S(2)}, u32[]{:S(2)}) collective-permute-start(bf16[2,64,4096]{2,1,0:T(8,128)(2,1)} %get-tuple-element.98), channel_id=1, source_target_pairs={{0,2},{1,3},{2,0},{3,1},{4,6},{5,7},{6,4},{7,5},{8,10},{9,11},{10,... | collective-permute-start | bytes 3145736 | tf_op jit(solution)/shard_map/ppermute | solution.py:129
  838.4 120.5 %collective-permute-start.11 = (bf16[2,64,4096]{2,1,0:T(8,128)(2,1)}, bf16[2,64,4096]{2,1,0:T(8,128)(2,1)}, u32[]{:S(2)}, u32[]{:S(2)}) collective-permute-start(bf16[2,64,4096]{2,1,0:T(8,128)(2,1)} %get-tuple-element.97), channel_id=1, source_target_pairs={{0,3},{1,2},{2,1},{3,0},{4,7},{5,6},{6,5},{7,4},{8,11},{9,10},{10,... | collective-permute-start | bytes 3145736 | tf_op jit(solution)/shard_map/ppermute | solution.py:129
  839.6 129.6 %collective-permute-start.9 = (bf16[2,64,4096]{2,1,0:T(8,128)(2,1)S(1)}, bf16[2,64,4096]{2,1,0:T(8,128)(2,1)}, u32[]{:S(2)}, u32[]{:S(2)}) collective-permute-start(bf16[2,64,4096]{2,1,0:T(8,128)(2,1)S(1)} %get-tuple-element.99), channel_id=1, source_target_pairs={{0,1},{1,0},{2,3},{3,2},{4,5},{5,4},{6,7},{7,6},{8,9},{9,8},{10,11... | collective-permute-start | bytes 3145736 | tf_op jit(solution)/shard_map/ppermute | solution.py:129
  1048.2 104.0 %all-to-all-start.3 = ((bf16[32,64,8,128]{3,2,1,0:T(8,128)(2,1)}), bf16[32,64,8,128]{3,2,1,0:T(8,128)(2,1)}, u32[]{:S(2)}, u32[]{:S(2)}) async-start(bf16[32,64,8,128]{3,2,1,0:T(8,128)(2,1)} %copy.368), calls=%async_computation.3 | async-start | bytes 8388608 | tf_op jit(solution)/shard_map/all_to_all | solution.py:172
  1185.4 68.6 %collective-permute-start.15 = (bf16[2,1024,512]{2,1,0:T(8,128)(2,1)}, bf16[2,1024,512]{2,1,0:T(8,128)(2,1)}, u32[]{:S(2)}, u32[]{:S(2)}) collective-permute-start(bf16[2,1024,512]{2,1,0:T(8,128)(2,1)} %constant_dynamic-slice_fusion.2), channel_id=1, source_target_pairs={{31,0},{0,1},{1,2},{2,3},{3,4},{4,5},{5,6},{6,7},{7,8},{8,9},{9,10... | collective-permute-start | bytes 6291464 | tf_op jit(solution)/shard_map/ppermute | solution.py:19
  1195.0 82.3 %collective-permute-start.16 = (bf16[2,1024,512]{2,1,0:T(8,128)(2,1)}, bf16[2,1024,512]{2,1,0:T(8,128)(2,1)}, u32[]{:S(2)}, u32[]{:S(2)}) collective-permute-start(bf16[2,1024,512]{2,1,0:T(8,128)(2,1)} %constant_dynamic-slice_fusion), channel_id=1, source_target_pairs={{1,0},{2,1},{3,2},{4,3},{5,4},{6,5},{7,6},{8,7},{9,8},{10,9},{11,1... | collective-permute-start | bytes 6291464 | tf_op jit(solution)/shard_map/ppermute | solution.py:19
  1212.0 65.3 %copy-start.5 = (f32[1024,1024]{1,0:T(8,128)S(1)}, f32[1024,1024]{1,0:T(8,128)}, u32[]{:S(2)}) copy-start(f32[1024,1024]{1,0:T(8,128)} %multiply_multiply_fusion) | copy-start | bytes 12582916
  (16 other events, 130.1 us)

commit v2 on v1

--- a/solution.py
+++ b/solution.py
@@ -9,7 +9,7 @@
 N = 16384
 FS = 1024
 SPLIT = 128
-PARTS = (1, 2, 2, 2, 1)
+PARTS = (1,) * 8
 AHEAD = 2
 
 
@@ -66,14 +66,14 @@
     turned = rotate((mixed[:, :lead_len], mixed[:, lead_len:]), twiddle_table(lead_len, SPLIT, N))
     section_one = jnp.concatenate([part.astype(jnp.bfloat16) for part in turned], axis=2)
     table = paired_table(SPLIT).transpose(1, 0, 2, 3).reshape(2 * SPLIT, 2 * SPLIT)
-    done = mix("kb,rpb->rkp", table, section_one).astype(jnp.bfloat16)
-    return done.reshape(row_count, devices, -1, lead_len).transpose(1, 0, 2, 3)
+    done = mix("kb,rpb->krp", table, section_one).astype(jnp.bfloat16)
+    return done.reshape(devices, -1, row_count, lead_len).transpose(0, 2, 1, 3)
 
 
 def strip_table(devices, spans):
     pairs = paired_table(devices)
     eye = jnp.eye(spans, dtype=jnp.bfloat16)
-    full = pairs.transpose(0, 1, 3, 2)[:, None, :, :, None, :] * eye[None, :, None, None, :, None]
+    full = pairs.transpose(0, 1, 3, 2)[:, :, None, :, None, :] * eye[None, None, :, None, :, None]
     return full.reshape(2 * spans * devices, devices, spans * 2)
 
 
@@ -119,35 +119,38 @@
     def fetch(place, after):
         here = my_col
         if after is not None:
-            here = lax.optimization_barrier((here, after))[0]
-        pieces = []
+            here = lax.optimization_barrier((here, *after))[0]
+        pieces, cut = [], []
         for hop in range(col_devices):
             sent = lax.dynamic_slice(
                 image, (0, here ^ hop, starts[place], 0), (2, 1, sizes[place], image.shape[3])
             )[:, 0]
+            cut.append(sent)
             if hop:
                 sent = lax.ppermute(sent, "col", [(i, i ^ hop) for i in range(col_devices)])
             pieces.append(sent)
-        return pieces
+        return pieces, cut
 
     strips = strip_table(devices, spans).reshape(2 * spans * devices, devices, -1)
 
     def columns_pass(columns, place):
-        mixed = mix("ugs,grsp->rup", strips, columns)
+        mixed = mix("ugs,grsp->urp", strips, columns)
         half = spans * devices
         band = slice(starts[place], starts[place] + sizes[place])
-        twiddle = tuple(jnp.tile(t[:, band].T, (1, spans))[:, :, None] for t in full_twiddle)
-        turned = rotate((mixed[:, :half], mixed[:, half:]), twiddle)
-        section_two = jnp.concatenate([part.astype(jnp.bfloat16) for part in turned], axis=0)
-        section_two = section_two.reshape(-1, spans, devices, lead_len)
+        twiddle = tuple(jnp.repeat(t[:, band], spans, axis=0)[:, :, None] for t in full_twiddle)
+        turned = rotate((mixed[:half], mixed[half:]), twiddle)
+        section_two = jnp.concatenate([part.astype(jnp.bfloat16) for part in turned], axis=1)
         return [
-            mix("km,mjpc->kpjc", t[:, :, band].reshape(t.shape[0], -1), section_two)
+            mix("km,zmc->kzc", t[:, :, band].reshape(t.shape[0], -1), section_two)
             for t in group_tables
         ]
 
     count = len(sizes)
     totals, spread, gate = None, [], None
-    queue = [fetch(0, None), fetch(1, None)]
+    queue, cut = [], None
+    for place in range(AHEAD):
+        pieces, cut = fetch(place, cut)
+        queue.append(pieces)
 
     def gather_columns(place, totals):
         columns = spread[place]
@@ -167,7 +170,8 @@
             shares, totals = lax.optimization_barrier((shares, totals))
         gate = shares
         if place + AHEAD < count:
-            queue.append(fetch(place + AHEAD, gate))
+            pieces, cut = fetch(place + AHEAD, (*cut, gate))
+            queue.append(pieces)
         spread.append(
             lax.all_to_all(shares, ("row", "col"), split_axis=0, concat_axis=0, tiled=True)
         )

time: 1300 us -> 1210 us (0.931)
  local copies, waits for them, and re-layouts: 227 us -> 168 us
  other arithmetic: 90.1 us -> 57.3 us
  starting transfers between devices: 69 us -> 89.6 us
  matrix products: 157 us -> 143 us
    convert_element_type x5 -> x0, local copies, waits for them, and re-layouts: 48.8 us -> none  [rows_pass(): done = mix('kb,rpb->rkp', table, section_one).astype(jnp.bfloat16)]
    all_to_all x5 -> x8, waiting for transfers between devices: 33.7 us -> 74 us  [shards(): lax.all_to_all(shares, ('row', 'col'), split_axis=0, concat_axis=0, tiled...]
    ppermute x15 -> x24, waiting for transfers between devices: 639 us -> 599 us  [fetch(): sent = lax.ppermute(sent, 'col', [(i, i ^ hop) for i in range(col_devices)])]
    concatenate x5 -> x8, other arithmetic: 27.2 us -> 2.91 us  [columns_pass(): jnp.concatenate([part.astype(jnp.bfloat16) for part in turned], axis=1)]
    reshape x5 -> x8, local copies, waits for them, and re-layouts: 48.9 us -> 25.3 us  [rows_pass(): return done.reshape(devices, -1, row_count, lead_len).transpose(0, 2, 1, 3)]
    optimization_barrier x3 -> x0, local copies, waits for them, and re-layouts: 21.3 us -> none  [shards(): shares, totals = lax.optimization_barrier((shares, totals))]
    mul x4 -> x20, local copies, waits for them, and re-layouts: 0.66 us -> 19.6 us  [the longest x8 8.47 us: rotate(): pair[0] * twiddle[0] - pair[1] * twiddle[1]]
    reshape x10 -> x16, local copies, waits for them, and re-layouts: 0.78 us -> 17.2 us  [columns_pass(): t[:, :, band].reshape(t.shape[0], -1)]
  transfers between devices with their start and end apart: 22 -> 34, of which waited for: 16 -> 25; matrix products, arithmetic and copies ran while one was open for 32% -> 27% of each run, Pallas kernels for 0% -> 0%
where the time goes in v2:
time: 1210 us; the launch traced here: 1200 us
  waiting for transfers between devices  737 us (61%)
  local copies, waits for them, and re-layouts  168 us (14%)
  matrix products  143 us (12%)
  starting transfers between devices  89.6 us (7%)
  other arithmetic  57.3 us (5%)
    ppermute x24, waiting for transfers between devices, fetch(): sent = lax.ppermute(sent, 'col', [(i, i ^ hop) for i in range(col_devices)])  599 us
    dot_general x40, matrix products, mix(): jnp.einsum(formula, table, values, preferred_element_type=jnp.float32)  143 us
    all_to_all x8, waiting for transfers between devices, shards(): lax.all_to_all(shares, ('row', 'col'), split_axis=0, concat_axis=0, tiled...  74 us
    all_to_all x8, starting transfers between devices, shards(): lax.all_to_all(shares, ('row', 'col'), split_axis=0, concat_axis=0, tiled...  65.1 us
    ppermute x2, waiting for transfers between devices, shifted(): return lax.ppermute(block, axis, route)  63.2 us
    unnamed x244, local copies, waits for them, and re-layouts  36.8 us
    squeeze x7, local copies, waits for them, and re-layouts, fetch(): lax.dynamic_slice(image, (0, here ^ hop, starts[place], 0), (2, 1, sizes[...  25.4 us
    reshape x8, local copies, waits for them, and re-layouts, rows_pass(): return done.reshape(devices, -1, row_count, lead_len).transpose(0, 2, 1, 3)  25.3 us
  transfers between devices with their start and end apart: 34, of which 25 were waited for; matrix products, arithmetic and copies ran while one was open for 27% of the time, Pallas kernels for 0%

profile of v2, /device:TPU:1, one launch (start us, length us, event | category | flops | bytes accessed | tf_op | source)
XLA Modules:
  0.0 1201.3 jit_solution(1138561510257296670)
XLA Ops:
  14.0 14.8 %collective-permute-done = bf16[2,64,4096]{2,1,0:T(8,128)(2,1)} collective-permute-done((bf16[2,64,4096]{2,1,0:T(8,128)(2,1)}, bf16[2,64,4096]{2,1,0:T(8,128)(2,1)}, u32[]{:S(2)}, u32[]{:S(2)}) %collective-permute-start) | collective-permute-done | bytes 1048608 | tf_op jit(solution)/shard_map/ppermute | solution.py:130
  31.7 20.5 %collective-permute-done.2 = bf16[2,64,4096]{2,1,0:T(8,128)(2,1)} collective-permute-done((bf16[2,64,4096]{2,1,0:T(8,128)(2,1)}, bf16[2,64,4096]{2,1,0:T(8,128)(2,1)}, u32[]{:S(2)}, u32[]{:S(2)}) %collective-permute-start.2) | collective-permute-done | bytes 1048608 | tf_op jit(solution)/shard_map/ppermute | solution.py:130
  61.0 8.3 all-to-all-start
  76.0 56.8 %collective-permute-done.3 = bf16[2,64,4096]{2,1,0:T(8,128)(2,1)S(1)} collective-permute-done((bf16[2,64,4096]{2,1,0:T(8,128)(2,1)}, bf16[2,64,4096]{2,1,0:T(8,128)(2,1)S(1)}, u32[]{:S(2)}, u32[]{:S(2)}) %collective-permute-start.3) | collective-permute-done | bytes 1048608 | tf_op jit(solution)/shard_map/ppermute | solution.py:130
  133.5 31.0 %collective-permute-done.5 = bf16[2,64,4096]{2,1,0:T(8,128)(2,1)S(1)} collective-permute-done((bf16[2,64,4096]{2,1,0:T(8,128)(2,1)S(1)}, bf16[2,64,4096]{2,1,0:T(8,128)(2,1)S(1)}, u32[]{:S(2)}, u32[]{:S(2)}) %collective-permute-start.5) | collective-permute-done | bytes 1048608 | tf_op jit(solution)/shard_map/ppermute | solution.py:130
  208.7 35.5 %collective-permute-done.6 = bf16[2,64,4096]{2,1,0:T(8,128)(2,1)} collective-permute-done((bf16[2,64,4096]{2,1,0:T(8,128)(2,1)}, bf16[2,64,4096]{2,1,0:T(8,128)(2,1)}, u32[]{:S(2)}, u32[]{:S(2)}) %collective-permute-start.6) | collective-permute-done | bytes 1048608 | tf_op jit(solution)/shard_map/ppermute | solution.py:130
  249.9 26.1 %collective-permute-done.8 = bf16[2,64,4096]{2,1,0:T(8,128)(2,1)} collective-permute-done((bf16[2,64,4096]{2,1,0:T(8,128)(2,1)S(1)}, bf16[2,64,4096]{2,1,0:T(8,128)(2,1)}, u32[]{:S(2)}, u32[]{:S(2)}) %collective-permute-start.8) | collective-permute-done | bytes 1048608 | tf_op jit(solution)/shard_map/ppermute | solution.py:130
  306.4 8.3 all-to-all-start.2
  329.0 77.7 %collective-permute-done.10 = bf16[2,64,4096]{2,1,0:T(8,128)(2,1)} collective-permute-done((bf16[2,64,4096]{2,1,0:T(8,128)(2,1)}, bf16[2,64,4096]{2,1,0:T(8,128)(2,1)}, u32[]{:S(2)}, u32[]{:S(2)}) %collective-permute-start.10) | collective-permute-done | bytes 1048608 | tf_op jit(solution)/shard_map/ppermute | solution.py:130
  441.4 8.3 all-to-all-start.3
  463.3 49.9 %collective-permute-done.12 = bf16[2,64,4096]{2,1,0:T(8,128)(2,1)} collective-permute-done((bf16[2,64,4096]{2,1,0:T(8,128)(2,1)}, bf16[2,64,4096]{2,1,0:T(8,128)(2,1)}, u32[]{:S(2)}, u32[]{:S(2)}) %collective-permute-start.12) | collective-permute-done | bytes 1048608 | tf_op jit(solution)/shard_map/ppermute | solution.py:130
  514.1 30.9 %collective-permute-done.14 = bf16[2,64,4096]{2,1,0:T(8,128)(2,1)} collective-permute-done((bf16[2,64,4096]{2,1,0:T(8,128)(2,1)S(1)}, bf16[2,64,4096]{2,1,0:T(8,128)(2,1)}, u32[]{:S(2)}, u32[]{:S(2)}) %collective-permute-start.14) | collective-permute-done | bytes 1048608 | tf_op jit(solution)/shard_map/ppermute | solution.py:130
  575.7 8.1 all-to-all-start.4
  597.6 49.8 %collective-permute-done.15 = bf16[2,64,4096]{2,1,0:T(8,128)(2,1)} collective-permute-done((bf16[2,64,4096]{2,1,0:T(8,128)(2,1)}, bf16[2,64,4096]{2,1,0:T(8,128)(2,1)}, u32[]{:S(2)}, u32[]{:S(2)}) %collective-permute-start.15) | collective-permute-done | bytes 1048608 | tf_op jit(solution)/shard_map/ppermute | solution.py:130
  648.2 30.9 %collective-permute-done.17 = bf16[2,64,4096]{2,1,0:T(8,128)(2,1)} collective-permute-done((bf16[2,64,4096]{2,1,0:T(8,128)(2,1)S(1)}, bf16[2,64,4096]{2,1,0:T(8,128)(2,1)}, u32[]{:S(2)}, u32[]{:S(2)}) %collective-permute-start.17) | collective-permute-done | bytes 1048608 | tf_op jit(solution)/shard_map/ppermute | solution.py:130
  731.6 49.9 %collective-permute-done.21 = bf16[2,64,4096]{2,1,0:T(8,128)(2,1)} collective-permute-done((bf16[2,64,4096]{2,1,0:T(8,128)(2,1)}, bf16[2,64,4096]{2,1,0:T(8,128)(2,1)}, u32[]{:S(2)}, u32[]{:S(2)}) %collective-permute-start.21) | collective-permute-done | bytes 1048608 | tf_op jit(solution)/shard_map/ppermute | solution.py:130
  782.4 30.9 %collective-permute-done.23 = bf16[2,64,4096]{2,1,0:T(8,128)(2,1)} collective-permute-done((bf16[2,64,4096]{2,1,0:T(8,128)(2,1)S(1)}, bf16[2,64,4096]{2,1,0:T(8,128)(2,1)}, u32[]{:S(2)}, u32[]{:S(2)}) %collective-permute-start.23) | collective-permute-done | bytes 1048608 | tf_op jit(solution)/shard_map/ppermute | solution.py:130
  844.0 8.1 all-to-all-start.7
  865.8 49.8 %collective-permute-done.18 = bf16[2,64,4096]{2,1,0:T(8,128)(2,1)} collective-permute-done((bf16[2,64,4096]{2,1,0:T(8,128)(2,1)}, bf16[2,64,4096]{2,1,0:T(8,128)(2,1)}, u32[]{:S(2)}, u32[]{:S(2)}) %collective-permute-start.18) | collective-permute-done | bytes 1048608 | tf_op jit(solution)/shard_map/ppermute | solution.py:130
  916.4 30.9 %collective-permute-done.20 = bf16[2,64,4096]{2,1,0:T(8,128)(2,1)} collective-permute-done((bf16[2,64,4096]{2,1,0:T(8,128)(2,1)S(1)}, bf16[2,64,4096]{2,1,0:T(8,128)(2,1)}, u32[]{:S(2)}, u32[]{:S(2)}) %collective-permute-start.20) | collective-permute-done | bytes 1048608 | tf_op jit(solution)/shard_map/ppermute | solution.py:130
  978.2 8.0 all-to-all-start.6
  1005.7 74.0 %all-to-all-done.6 = bf16[32,64,8,128]{3,2,1,0:T(8,128)(2,1)} async-done(((bf16[32,64,8,128]{3,2,1,0:T(8,128)(2,1)}), bf16[32,64,8,128]{3,2,1,0:T(8,128)(2,1)}, u32[]{:S(2)}, u32[]{:S(2)}) %all-to-all-start.6) | async-done | bytes 4194336 | tf_op jit(solution)/shard_map/all_to_all | solution.py:176
  1130.4 39.9 %collective-permute-done.24 = bf16[2,1024,512]{2,1,0:T(8,128)(2,1)} collective-permute-done((bf16[2,1024,512]{2,1,0:T(8,128)(2,1)}, bf16[2,1024,512]{2,1,0:T(8,128)(2,1)}, u32[]{:S(2)}, u32[]{:S(2)}) %collective-permute-start.24) | collective-permute-done | bytes 2097184 | tf_op jit(solution)/shard_map/ppermute | solution.py:19
  1170.3 23.3 %collective-permute-done.25 = bf16[2,1024,512]{2,1,0:T(8,128)(2,1)} collective-permute-done((bf16[2,1024,512]{2,1,0:T(8,128)(2,1)}, bf16[2,1024,512]{2,1,0:T(8,128)(2,1)}, u32[]{:S(2)}, u32[]{:S(2)}) %collective-permute-start.25) | collective-permute-done | bytes 2097184 | tf_op jit(solution)/shard_map/ppermute | solution.py:19
  (483 shorter events, 422.9 us)
Async XLA Ops:
  61.0 111.8 %all-to-all-start = ((bf16[32,64,8,128]{3,2,1,0:T(8,128)(2,1)}), bf16[32,64,8,128]{3,2,1,0:T(8,128)(2,1)}, u32[]{:S(2)}, u32[]{:S(2)}) async-start(bf16[32,64,8,128]{3,2,1,0:T(8,128)(2,1)} %bitcast.568), calls=%async_computation | async-start | bytes 8388608 | tf_op jit(solution)/shard_map/all_to_all | solution.py:176
  69.2 63.5 %collective-permute-start.3 = (bf16[2,64,4096]{2,1,0:T(8,128)(2,1)}, bf16[2,64,4096]{2,1,0:T(8,128)(2,1)S(1)}, u32[]{:S(2)}, u32[]{:S(2)}) collective-permute-start(bf16[2,64,4096]{2,1,0:T(8,128)(2,1)} %get-tuple-element.184), channel_id=1, source_target_pairs={{0,1},{1,0},{2,3},{3,2},{4,5},{5,4},{6,7},{7,6},{8,9},{9,8},{10,11... | collective-permute-start | bytes 3145736 | tf_op jit(solution)/shard_map/ppermute | solution.py:130
  70.7 62.9 %collective-permute-start.4 = (bf16[2,64,4096]{2,1,0:T(8,128)(2,1)S(1)}, bf16[2,64,4096]{2,1,0:T(8,128)(2,1)S(1)}, u32[]{:S(2)}, u32[]{:S(2)}) collective-permute-start(bf16[2,64,4096]{2,1,0:T(8,128)(2,1)S(1)} %get-tuple-element.183), channel_id=1, source_target_pairs={{0,2},{1,3},{2,0},{3,1},{4,6},{5,7},{6,4},{7,5},{8,10},{9,11},{10,... | collective-permute-start | bytes 3145736 | tf_op jit(solution)/shard_map/ppermute | solution.py:130
  71.8 92.7 %collective-permute-start.5 = (bf16[2,64,4096]{2,1,0:T(8,128)(2,1)S(1)}, bf16[2,64,4096]{2,1,0:T(8,128)(2,1)S(1)}, u32[]{:S(2)}, u32[]{:S(2)}) collective-permute-start(bf16[2,64,4096]{2,1,0:T(8,128)(2,1)S(1)} %get-tuple-element.182), channel_id=1, source_target_pairs={{0,3},{1,2},{2,1},{3,0},{4,7},{5,6},{6,5},{7,4},{8,11},{9,10},{10,... | collective-permute-start | bytes 3145736 | tf_op jit(solution)/shard_map/ppermute | solution.py:130
  172.7 133.7 %all-to-all-start.1 = ((bf16[32,64,8,128]{3,2,1,0:T(8,128)(2,1)}), bf16[32,64,8,128]{3,2,1,0:T(8,128)(2,1)}, u32[]{:S(2)}, u32[]{:S(2)}) async-start(bf16[32,64,8,128]{3,2,1,0:T(8,128)(2,1)} %bitcast.561), calls=%async_computation.1 | async-start | bytes 8388608 | tf_op jit(solution)/shard_map/all_to_all | solution.py:176
  191.3 84.7 %collective-permute-start.8 = (bf16[2,64,4096]{2,1,0:T(8,128)(2,1)S(1)}, bf16[2,64,4096]{2,1,0:T(8,128)(2,1)}, u32[]{:S(2)}, u32[]{:S(2)}) collective-permute-start(bf16[2,64,4096]{2,1,0:T(8,128)(2,1)S(1)} %get-tuple-element.177), channel_id=1, source_target_pairs={{0,3},{1,2},{2,1},{3,0},{4,7},{5,6},{6,5},{7,4},{8,11},{9,10},{10,... | collective-permute-start | bytes 3145736 | tf_op jit(solution)/shard_map/ppermute | solution.py:130
  306.4 135.0 %all-to-all-start.2 = ((bf16[32,64,8,128]{3,2,1,0:T(8,128)(2,1)}), bf16[32,64,8,128]{3,2,1,0:T(8,128)(2,1)}, u32[]{:S(2)}, u32[]{:S(2)}) async-start(bf16[32,64,8,128]{3,2,1,0:T(8,128)(2,1)} %bitcast.565), calls=%async_computation.2 | async-start | bytes 8388608 | tf_op jit(solution)/shard_map/all_to_all | solution.py:176
  318.3 88.5 %collective-permute-start.10 = (bf16[2,64,4096]{2,1,0:T(8,128)(2,1)}, bf16[2,64,4096]{2,1,0:T(8,128)(2,1)}, u32[]{:S(2)}, u32[]{:S(2)}) collective-permute-start(bf16[2,64,4096]{2,1,0:T(8,128)(2,1)} %get-tuple-element.174), channel_id=1, source_target_pairs={{0,2},{1,3},{2,0},{3,1},{4,6},{5,7},{6,4},{7,5},{8,10},{9,11},{10,... | collective-permute-start | bytes 3145736 | tf_op jit(solution)/shard_map/ppermute | solution.py:130
  319.6 87.1 %collective-permute-start.11 = (bf16[2,64,4096]{2,1,0:T(8,128)(2,1)S(1)}, bf16[2,64,4096]{2,1,0:T(8,128)(2,1)}, u32[]{:S(2)}, u32[]{:S(2)}) collective-permute-start(bf16[2,64,4096]{2,1,0:T(8,128)(2,1)S(1)} %get-tuple-element.173), channel_id=1, source_target_pairs={{0,3},{1,2},{2,1},{3,0},{4,7},{5,6},{6,5},{7,4},{8,11},{9,10},{10,... | collective-permute-start | bytes 3145736 | tf_op jit(solution)/shard_map/ppermute | solution.py:130
  320.8 90.0 %collective-permute-start.9 = (bf16[2,64,4096]{2,1,0:T(8,128)(2,1)S(1)}, bf16[2,64,4096]{2,1,0:T(8,128)(2,1)}, u32[]{:S(2)}, u32[]{:S(2)}) collective-permute-start(bf16[2,64,4096]{2,1,0:T(8,128)(2,1)S(1)} %get-tuple-element.175), channel_id=1, source_target_pairs={{0,1},{1,0},{2,3},{3,2},{4,5},{5,4},{6,7},{7,6},{8,9},{9,8},{10,11... | collective-permute-start | bytes 3145736 | tf_op jit(solution)/shard_map/ppermute | solution.py:130
  441.4 134.2 %all-to-all-start.3 = ((bf16[32,64,8,128]{3,2,1,0:T(8,128)(2,1)}), bf16[32,64,8,128]{3,2,1,0:T(8,128)(2,1)}, u32[]{:S(2)}, u32[]{:S(2)}) async-start(bf16[32,64,8,128]{3,2,1,0:T(8,128)(2,1)} %bitcast.563), calls=%async_computation.3 | async-start | bytes 8388608 | tf_op jit(solution)/shard_map/all_to_all | solution.py:176
  453.3 60.0 %collective-permute-start.12 = (bf16[2,64,4096]{2,1,0:T(8,128)(2,1)}, bf16[2,64,4096]{2,1,0:T(8,128)(2,1)}, u32[]{:S(2)}, u32[]{:S(2)}) collective-permute-start(bf16[2,64,4096]{2,1,0:T(8,128)(2,1)} %get-tuple-element.171), channel_id=1, source_target_pairs={{0,1},{1,0},{2,3},{3,2},{4,5},{5,4},{6,7},{7,6},{8,9},{9,8},{10,11... | collective-permute-start | bytes 3145736 | tf_op jit(solution)/shard_map/ppermute | solution.py:130
  455.8 89.2 %collective-permute-start.14 = (bf16[2,64,4096]{2,1,0:T(8,128)(2,1)S(1)}, bf16[2,64,4096]{2,1,0:T(8,128)(2,1)}, u32[]{:S(2)}, u32[]{:S(2)}) collective-permute-start(bf16[2,64,4096]{2,1,0:T(8,128)(2,1)S(1)} %get-tuple-element.169), channel_id=1, source_target_pairs={{0,3},{1,2},{2,1},{3,0},{4,7},{5,6},{6,5},{7,4},{8,11},{9,10},{10,... | collective-permute-start | bytes 3145736 | tf_op jit(solution)/shard_map/ppermute | solution.py:130
  575.7 134.3 %all-to-all-start.4 = ((bf16[32,64,8,128]{3,2,1,0:T(8,128)(2,1)}), bf16[32,64,8,128]{3,2,1,0:T(8,128)(2,1)}, u32[]{:S(2)}, u32[]{:S(2)}) async-start(bf16[32,64,8,128]{3,2,1,0:T(8,128)(2,1)} %bitcast.564), calls=%async_computation.4 | async-start | bytes 8388608 | tf_op jit(solution)/shard_map/all_to_all | solution.py:176
  587.5 59.9 %collective-permute-start.15 = (bf16[2,64,4096]{2,1,0:T(8,128)(2,1)}, bf16[2,64,4096]{2,1,0:T(8,128)(2,1)}, u32[]{:S(2)}, u32[]{:S(2)}) collective-permute-start(bf16[2,64,4096]{2,1,0:T(8,128)(2,1)} %get-tuple-element.167), channel_id=1, source_target_pairs={{0,1},{1,0},{2,3},{3,2},{4,5},{5,4},{6,7},{7,6},{8,9},{9,8},{10,11... | collective-permute-start | bytes 3145736 | tf_op jit(solution)/shard_map/ppermute | solution.py:130
  590.0 89.1 %collective-permute-start.17 = (bf16[2,64,4096]{2,1,0:T(8,128)(2,1)S(1)}, bf16[2,64,4096]{2,1,0:T(8,128)(2,1)}, u32[]{:S(2)}, u32[]{:S(2)}) collective-permute-start(bf16[2,64,4096]{2,1,0:T(8,128)(2,1)S(1)} %get-tuple-element.165), channel_id=1, source_target_pairs={{0,3},{1,2},{2,1},{3,0},{4,7},{5,6},{6,5},{7,4},{8,11},{9,10},{10,... | collective-permute-start | bytes 3145736 | tf_op jit(solution)/shard_map/ppermute | solution.py:130
  710.0 133.9 %all-to-all-start.5 = ((bf16[32,64,8,128]{3,2,1,0:T(8,128)(2,1)}), bf16[32,64,8,128]{3,2,1,0:T(8,128)(2,1)}, u32[]{:S(2)}, u32[]{:S(2)}) async-start(bf16[32,64,8,128]{3,2,1,0:T(8,128)(2,1)} %bitcast.562), calls=%async_computation.5 | async-start | bytes 8388608 | tf_op jit(solution)/shard_map/all_to_all | solution.py:176
  721.6 60.0 %collective-permute-start.21 = (bf16[2,64,4096]{2,1,0:T(8,128)(2,1)}, bf16[2,64,4096]{2,1,0:T(8,128)(2,1)}, u32[]{:S(2)}, u32[]{:S(2)}) collective-permute-start(bf16[2,64,4096]{2,1,0:T(8,128)(2,1)} %get-tuple-element.163), channel_id=1, source_target_pairs={{0,1},{1,0},{2,3},{3,2},{4,5},{5,4},{6,7},{7,6},{8,9},{9,8},{10,11... | collective-permute-start | bytes 3145736 | tf_op jit(solution)/shard_map/ppermute | solution.py:130
  724.1 89.2 %collective-permute-start.23 = (bf16[2,64,4096]{2,1,0:T(8,128)(2,1)S(1)}, bf16[2,64,4096]{2,1,0:T(8,128)(2,1)}, u32[]{:S(2)}, u32[]{:S(2)}) collective-permute-start(bf16[2,64,4096]{2,1,0:T(8,128)(2,1)S(1)} %get-tuple-element.161), channel_id=1, source_target_pairs={{0,3},{1,2},{2,1},{3,0},{4,7},{5,6},{6,5},{7,4},{8,11},{9,10},{10,... | collective-permute-start | bytes 3145736 | tf_op jit(solution)/shard_map/ppermute | solution.py:130
  844.0 134.3 %all-to-all-start.7 = ((bf16[32,64,8,128]{3,2,1,0:T(8,128)(2,1)}), bf16[32,64,8,128]{3,2,1,0:T(8,128)(2,1)}, u32[]{:S(2)}, u32[]{:S(2)}) async-start(bf16[32,64,8,128]{3,2,1,0:T(8,128)(2,1)} %bitcast.566), calls=%async_computation.7 | async-start | bytes 8388608 | tf_op jit(solution)/shard_map/all_to_all | solution.py:176
  858.2 89.1 %collective-permute-start.20 = (bf16[2,64,4096]{2,1,0:T(8,128)(2,1)S(1)}, bf16[2,64,4096]{2,1,0:T(8,128)(2,1)}, u32[]{:S(2)}, u32[]{:S(2)}) collective-permute-start(bf16[2,64,4096]{2,1,0:T(8,128)(2,1)S(1)} %get-tuple-element.157), channel_id=1, source_target_pairs={{0,3},{1,2},{2,1},{3,0},{4,7},{5,6},{6,5},{7,4},{8,11},{9,10},{10,... | collective-permute-start | bytes 3145736 | tf_op jit(solution)/shard_map/ppermute | solution.py:130
  978.2 101.4 %all-to-all-start.6 = ((bf16[32,64,8,128]{3,2,1,0:T(8,128)(2,1)}), bf16[32,64,8,128]{3,2,1,0:T(8,128)(2,1)}, u32[]{:S(2)}, u32[]{:S(2)}) async-start(bf16[32,64,8,128]{3,2,1,0:T(8,128)(2,1)} %bitcast.567), calls=%async_computation.6 | async-start | bytes 8388608 | tf_op jit(solution)/shard_map/all_to_all | solution.py:176
  1101.7 68.6 %collective-permute-start.24 = (bf16[2,1024,512]{2,1,0:T(8,128)(2,1)}, bf16[2,1024,512]{2,1,0:T(8,128)(2,1)}, u32[]{:S(2)}, u32[]{:S(2)}) collective-permute-start(bf16[2,1024,512]{2,1,0:T(8,128)(2,1)} %constant_dynamic-slice_fusion.2), channel_id=1, source_target_pairs={{31,0},{0,1},{1,2},{2,3},{3,4},{4,5},{5,6},{6,7},{7,8},{8,9},{9,10... | collective-permute-start | bytes 6291464 | tf_op jit(solution)/shard_map/ppermute | solution.py:19
  1109.9 83.7 %collective-permute-start.25 = (bf16[2,1024,512]{2,1,0:T(8,128)(2,1)}, bf16[2,1024,512]{2,1,0:T(8,128)(2,1)}, u32[]{:S(2)}, u32[]{:S(2)}) collective-permute-start(bf16[2,1024,512]{2,1,0:T(8,128)(2,1)} %constant_dynamic-slice_fusion), channel_id=1, source_target_pairs={{1,0},{2,1},{3,2},{4,3},{5,4},{6,5},{7,6},{8,7},{9,8},{10,9},{11,1... | collective-permute-start | bytes 6291464 | tf_op jit(solution)/shard_map/ppermute | solution.py:19
  (116 other events, 1319.1 us)
